TPU v7x, 32 devices: a whole 2x2x4 slice. The times are simulated.
32 devices in a mesh: grp: 1, tm: 8 (over y, x, core), op: 4 (over z).
Axes of the slice: x: 2, y: 2, z: 4, core: 2. Of those that a mesh axis runs over, the one named last changes fastest.
Arguments:
- sources: bfloat16 [8, 16, 2, 384, 384], P(('grp', 'tm'), 'op'), may hold values from -6 to 6
- sink: bfloat16 [8, 2, 384, 384], P(('grp', 'tm')), may hold values from -0.3125 to 0.3125
- phase: float32 [8, 384], replicated, may hold values from -3.140625 to 3.140625
- task_table: int32 [3, 8, 16], P(None, ('grp', 'tm'), 'op'), may hold values from -1 to 15, as said below
Outputs:
- task_values: float32 [8, 16, 2, 384], P(('grp', 'tm'), 'op')
Inputs may be any that keep to these rules, and one draw needn't show every extreme that they name: `task_table`: field 0 lies in 0 to 15, field 1 in 0 to 7, field 2 is -1 (dead slot) or a rank 0 to 1. At each time slice, for every owner s exactly 2 homes have slot s live, and their places are 0 to 1, each once. At each time slice one home has all 4 slots live.
All inputs are finite; a program needn't handle non-finite values.
Results may differ from a plain program's by a relative error of at most 0.004.
Values may be sent and summed in bfloat16 or wider, within the bound.
No kernel may reach another device: no remote copies, remote signals or barrier semaphores. Data moves between devices by JAX's collectives and lax.ppermute only.
A program may use at most 64 MiB of HBM per device.

v0:
```python
import jax
import jax.numpy as jnp
from jax import lax
from jax.sharding import PartitionSpec as P

SEPARATIONS = (-2, -1, 1, 2)


def shifted_2(shard, axis, by):
    length = lax.axis_size(axis)
    return lax.ppermute(shard, axis, [(i, (i + by) % length) for i in range(length)])


def task_value(source, angle, sink_slice):
    blocks = jnp.einsum("xij,yjl->xyil", source, sink_slice, preferred_element_type=jnp.float32)
    quark_real = blocks[0, 0] - blocks[1, 1]
    quark_imag = blocks[0, 1] + blocks[1, 0]
    cosine = jnp.cos(angle)[None, :]
    sine = jnp.sin(angle)[None, :]
    phased = jnp.stack(
        [quark_real * cosine - quark_imag * sine, quark_real * sine + quark_imag * cosine]
    )
    phased = phased.astype(jnp.bfloat16)
    second = jnp.einsum("xil,yjl->xyij", phased, sink_slice, preferred_element_type=jnp.float32)
    loop_real = second[0, 0] + second[1, 1]
    loop_imag = second[1, 0] - second[0, 1]
    diag_real = jnp.sum(loop_real * loop_real.T - loop_imag * loop_imag.T, axis=1)
    diag_imag = jnp.sum(loop_real * loop_imag.T + loop_imag * loop_real.T, axis=1)
    return jnp.stack([diag_real, diag_imag]) / loop_real.shape[0]


def contract(chosen, angles, sink_slice):

    def single(pair):
        return task_value(pair[0], pair[1], sink_slice)

    return lax.map(single, (chosen, angles))


def angle_rows(moment_values, phase):
    levels = jnp.arange(phase.shape[0], dtype=jnp.float32)
    onehot = (moment_values[:, None] == levels[None, :]).astype(jnp.float32)
    return jnp.dot(
        onehot, phase, precision=lax.Precision.HIGHEST, preferred_element_type=jnp.float32
    )


def shards(sources, sink, phase, task_table):
    slab = sources[0]
    sink_slice = sink[0]
    shifted = {}
    for direction in (1, -1):
        current = slab
        for distance in (1, 2):
            current = shifted_2(current, "tm", -direction)
            shifted[direction * distance] = current
    stacked = jnp.concatenate([shifted[offset] for offset in SEPARATIONS], axis=0)
    picks = task_table[0, 0]
    moments = task_table[1, 0]
    places = task_table[2, 0]
    chosen = jnp.take(stacked, picks, axis=0)
    angles = angle_rows(moments.astype(jnp.float32), phase)
    live = (places >= 0).astype(jnp.float32)
    values = contract(chosen, angles, sink_slice) * live[:, None, None]
    return values[None]


def solution(mesh):
    return jax.shard_map(
        shards,
        mesh=mesh,
        in_specs=(
            P(("grp", "tm"), "op", None, None, None),
            P(("grp", "tm"), None, None, None),
            P(),
            P(None, ("grp", "tm"), "op"),
        ),
        out_specs=P(("grp", "tm"), "op", None, None),
        check_vma=False,
    )
```

profile of v0, /device:TPU:1, one launch (start us, length us, event | category | flops | bytes accessed | tf_op | source)
XLA Modules:
  0.0 148.4 jit_solution(13922783928232581761)
XLA Ops:
  0.0 2.6 %collective-permute-start = (bf16[4,2,384,384]{3,2,1,0:T(8,128)(2,1)}, bf16[4,2,384,384]{3,2,1,0:T(8,128)(2,1)S(1)}, u32[]{:S(2)}, u32[]{:S(2)}) collective-permute-start(bf16[4,2,384,384]{3,2,1,0:T(8,128)(2,1)} %bitcast.95), channel_id=1, source_target_pairs={{0,4},{4,8},{8,12},{12,16},{16,20},{20,24},{24,28},{28,0},{1,5},{5... | collective-permute-start | bytes 7077896 | tf_op jit(solution)/shard_map/ppermute | solution.py:11
  2.6 50.3 %collective-permute-done = bf16[4,2,384,384]{3,2,1,0:T(8,128)(2,1)S(1)} collective-permute-done((bf16[4,2,384,384]{3,2,1,0:T(8,128)(2,1)}, bf16[4,2,384,384]{3,2,1,0:T(8,128)(2,1)S(1)}, u32[]{:S(2)}, u32[]{:S(2)}) %collective-permute-start) | collective-permute-done | bytes 2359328 | tf_op jit(solution)/shard_map/ppermute | solution.py:11
  52.9 2.4 %collective-permute-start.1 = (bf16[4,2,384,384]{3,2,1,0:T(8,128)(2,1)S(1)}, bf16[4,2,384,384]{3,2,1,0:T(8,128)(2,1)}, u32[]{:S(2)}, u32[]{:S(2)}) collective-permute-start(bf16[4,2,384,384]{3,2,1,0:T(8,128)(2,1)S(1)} %collective-permute-done), channel_id=1, source_target_pairs={{0,4},{4,8},{8,12},{12,16},{16,20},{20,24},{24,28},{28,0},{1,5},{5... | collective-permute-start | bytes 7077896 | tf_op jit(solution)/shard_map/ppermute | solution.py:11
  56.3 0.7 compare_and_fusion
  58.3 0.8 fusion.16
  59.1 45.1 %collective-permute-done.1 = bf16[4,2,384,384]{3,2,1,0:T(8,128)(2,1)} collective-permute-done((bf16[4,2,384,384]{3,2,1,0:T(8,128)(2,1)S(1)}, bf16[4,2,384,384]{3,2,1,0:T(8,128)(2,1)}, u32[]{:S(2)}, u32[]{:S(2)}) %collective-permute-start.1) | collective-permute-done | bytes 2359328 | tf_op jit(solution)/shard_map/ppermute | solution.py:11
  104.1 5.1 %collective-permute-done.3 = bf16[4,2,384,384]{3,2,1,0:T(8,128)(2,1)} collective-permute-done((bf16[4,2,384,384]{3,2,1,0:T(8,128)(2,1)}, bf16[4,2,384,384]{3,2,1,0:T(8,128)(2,1)}, u32[]{:S(2)}, u32[]{:S(2)}) %collective-permute-start.3) | collective-permute-done | bytes 2359328 | tf_op jit(solution)/shard_map/ppermute | solution.py:11
  109.2 8.4 %pad_maximum_fusion = bf16[16,2,384,384]{3,2,1,0:T(8,128)(2,1)} fusion(bf16[4,2,384,384]{3,2,1,0:T(8,128)(2,1)} %collective-permute-done.3, bf16[4,2,384,384]{3,2,1,0:T(8,128)(2,1)} %collective-permute-done.2, bf16[4,2,384,384]{3,2,1,0:T(8,128)(2,1)S(1)} %collective-permute-done, bf16[4,2,384,384]{3,2,1,0:T(8,128)(2,1)} %collective-permute-done.1), kind=kLoop, calls=%fused_computation.34 | loop fusion | flops 14155776 | bytes 18874368 | tf_op jit(solution)/shard_map/concatenate | solution.py:57
  117.6 4.7 %gather_fusion = bf16[4,2,384,384]{3,2,1,0:T(8,128)(2,1)S(1)} fusion(bf16[16,2,384,384]{3,2,1,0:T(8,128)(2,1)} %pad_maximum_fusion, s32[1024]{0:T(1024)S(1)} %pad_clamp_fusion), kind=kCustom, calls=%fused_computation | custom fusion | bytes 4718608 | tf_op jit(solution)/shard_map/jit(_take)/gather | solution.py:61
  122.4 1.7 %broadcast_select_fusion = bf16[4,2,384,384]{3,2,1,0:T(8,128)(2,1)} fusion(bf16[4,2,384,384]{3,2,1,0:T(8,128)(2,1)S(1)} %gather_fusion, pred[4]{0:T(512)(128)(4,1)S(1)} %compare_and_fusion), kind=kLoop, calls=%fused_computation.35 | loop fusion | flops 1179648 | bytes 4718596 | tf_op jit(solution)/shard_map/jit(_take)/select_n | solution.py:61
  124.1 22.9 %while.10 = (s32[]{:T(128)}, f32[4,2,384]{2,1,0:T(2,128)}, bf16[4,2,384,384]{3,2,1,0:T(8,128)(2,1)}, bf16[2,384,384]{2,1,0:T(8,128)(2,1)S(1)}, f32[4,384]{1,0:T(4,128)}, /*index=5*/s32[]{:T(128)}) while((s32[]{:T(128)}, f32[4,2,384]{2,1,0:T(2,128)}, bf16[4,2,384,384]{3,2,1,0:T(8,128)(2,1)}, bf16[2,384,384]{2,1,0:T(8,128)(2,1)S(1)}, ...), condition=%wide.region_3.4_spmd, body=%wide.region_0.3_spmd.sunk | while | flops 910246656 | bytes 23617096 | solution.py:37
  124.1 1.8 %convolution_bitcast_fusion.4 = f32[2,2,384,384]{3,2,1,0:T(8,128)S(1)} fusion(bf16[2,384,384]{2,1,0:T(8,128)(2,1)S(1)} %get-tuple-element.116, bf16[4,2,384,384]{3,2,1,0:T(8,128)(2,1)} %get-tuple-element.115, s32[]{:T(128)} %get-tuple-element.107), kind=kOutput, calls=%fused_computation.2.clone.1 | convolution fusion | flops 452984832 | bytes 3539456 | tf_op jit(solution)/shard_map/while/body/eval_jaxpr/xij,yjl->xyil/dot_general | solution.py:15
  126.0 0.8 cosine_reduce_fusion.2
  126.9 0.8 convolution_bitcast_fusion.5
  129.8 1.8 %convolution_bitcast_fusion.4 = f32[2,2,384,384]{3,2,1,0:T(8,128)S(1)} fusion(bf16[2,384,384]{2,1,0:T(8,128)(2,1)S(1)} %get-tuple-element.116, bf16[4,2,384,384]{3,2,1,0:T(8,128)(2,1)} %get-tuple-element.115, s32[]{:T(128)} %get-tuple-element.107), kind=kOutput, calls=%fused_computation.2.clone.1 | convolution fusion | flops 452984832 | bytes 3539456 | tf_op jit(solution)/shard_map/while/body/eval_jaxpr/xij,yjl->xyil/dot_general | solution.py:15
  131.7 0.8 cosine_reduce_fusion.2
  132.7 0.8 convolution_bitcast_fusion.5
  135.5 1.8 %convolution_bitcast_fusion.4 = f32[2,2,384,384]{3,2,1,0:T(8,128)S(1)} fusion(bf16[2,384,384]{2,1,0:T(8,128)(2,1)S(1)} %get-tuple-element.116, bf16[4,2,384,384]{3,2,1,0:T(8,128)(2,1)} %get-tuple-element.115, s32[]{:T(128)} %get-tuple-element.107), kind=kOutput, calls=%fused_computation.2.clone.1 | convolution fusion | flops 452984832 | bytes 3539456 | tf_op jit(solution)/shard_map/while/body/eval_jaxpr/xij,yjl->xyil/dot_general | solution.py:15
  137.4 0.8 cosine_reduce_fusion.2
  138.4 0.8 convolution_bitcast_fusion.5
  141.3 1.8 %convolution_bitcast_fusion.4 = f32[2,2,384,384]{3,2,1,0:T(8,128)S(1)} fusion(bf16[2,384,384]{2,1,0:T(8,128)(2,1)S(1)} %get-tuple-element.116, bf16[4,2,384,384]{3,2,1,0:T(8,128)(2,1)} %get-tuple-element.115, s32[]{:T(128)} %get-tuple-element.107), kind=kOutput, calls=%fused_computation.2.clone.1 | convolution fusion | flops 452984832 | bytes 3539456 | tf_op jit(solution)/shard_map/while/body/eval_jaxpr/xij,yjl->xyil/dot_general | solution.py:15
  143.1 0.8 cosine_reduce_fusion.2
  144.1 0.8 convolution_bitcast_fusion.5
  147.0 1.4 multiply_bitcast_fusion
  (56 shorter events, 11.4 us)
Async XLA Ops:
  0.0 58.3 %copy-start = (f32[8,384]{1,0:T(8,128)S(1)}, f32[8,384]{1,0:T(8,128)}, u32[]{:S(2)}) copy-start(f32[8,384]{1,0:T(8,128)} %param.8) | copy-start | bytes 36868
  0.0 52.9 %collective-permute-start = (bf16[4,2,384,384]{3,2,1,0:T(8,128)(2,1)}, bf16[4,2,384,384]{3,2,1,0:T(8,128)(2,1)S(1)}, u32[]{:S(2)}, u32[]{:S(2)}) collective-permute-start(bf16[4,2,384,384]{3,2,1,0:T(8,128)(2,1)} %bitcast.95), channel_id=1, source_target_pairs={{0,4},{4,8},{8,12},{12,16},{16,20},{20,24},{24,28},{28,0},{1,5},{5... | collective-permute-start | bytes 7077896 | tf_op jit(solution)/shard_map/ppermute | solution.py:11
  2.6 53.0 %collective-permute-start.2 = (bf16[4,2,384,384]{3,2,1,0:T(8,128)(2,1)}, bf16[4,2,384,384]{3,2,1,0:T(8,128)(2,1)}, u32[]{:S(2)}, u32[]{:S(2)}) collective-permute-start(bf16[4,2,384,384]{3,2,1,0:T(8,128)(2,1)} %bitcast.96), channel_id=1, source_target_pairs={{0,28},{4,0},{8,4},{12,8},{16,12},{20,16},{24,20},{28,24},{1,29},{... | collective-permute-start | bytes 7077896 | tf_op jit(solution)/shard_map/ppermute | solution.py:11
  52.9 51.2 %collective-permute-start.1 = (bf16[4,2,384,384]{3,2,1,0:T(8,128)(2,1)S(1)}, bf16[4,2,384,384]{3,2,1,0:T(8,128)(2,1)}, u32[]{:S(2)}, u32[]{:S(2)}) collective-permute-start(bf16[4,2,384,384]{3,2,1,0:T(8,128)(2,1)S(1)} %collective-permute-done), channel_id=1, source_target_pairs={{0,4},{4,8},{8,12},{12,16},{16,20},{20,24},{24,28},{28,0},{1,5},{5... | collective-permute-start | bytes 7077896 | tf_op jit(solution)/shard_map/ppermute | solution.py:11
  55.6 53.6 %collective-permute-start.3 = (bf16[4,2,384,384]{3,2,1,0:T(8,128)(2,1)}, bf16[4,2,384,384]{3,2,1,0:T(8,128)(2,1)}, u32[]{:S(2)}, u32[]{:S(2)}) collective-permute-start(bf16[4,2,384,384]{3,2,1,0:T(8,128)(2,1)} %collective-permute-done.2), channel_id=1, source_target_pairs={{0,28},{4,0},{8,4},{12,8},{16,12},{20,16},{24,20},{28,24},{1,29},{... | collective-permute-start | bytes 7077896 | tf_op jit(solution)/shard_map/ppermute | solution.py:11
  122.4 1.8 %copy-start.1 = (bf16[1,2,384,384]{3,2,1,0:T(8,128)(2,1)S(1)}, bf16[1,2,384,384]{3,2,1,0:T(8,128)(2,1)}, u32[]{:S(2)}) copy-start(bf16[1,2,384,384]{3,2,1,0:T(8,128)(2,1)} %param.7) | copy-start | bytes 1769476
where the time goes:
time: 149 us; the launch traced here: 148 us
  waiting for transfers between devices  101 us (68%)
  other arithmetic  19.5 us (13%)
  local copies, waits for them, and re-layouts  11.6 us (8%)
  matrix products  11.3 us (8%)
  starting transfers between devices  4.97 us (3%)
    ppermute x4, waiting for transfers between devices, shifted_2(): lax.ppermute(shard, axis, [(i, (i + by) % length) for i in range(length)])  101 us
    concatenate x1, other arithmetic, shards(): jnp.concatenate([shifted[offset] for offset in SEPARATIONS], axis=0)  8.36 us
    dot_general x4, matrix products, task_value(): jnp.einsum('xij,yjl->xyil', source, sink_slice, preferred_element_type=jn...  7.34 us
    ppermute x4, starting transfers between devices, shifted_2(): lax.ppermute(shard, axis, [(i, (i + by) % length) for i in range(length)])  4.97 us
    gather x1, local copies, waits for them, and re-layouts, shards(): chosen = jnp.take(stacked, picks, axis=0)  4.75 us
    dot_general x4, matrix products, task_value(): jnp.einsum('xil,yjl->xyij', phased, sink_slice, preferred_element_type=jn...  3.2 us
    cos x4, local copies, waits for them, and re-layouts, task_value(): cosine = jnp.cos(angle)[None, :]  3.09 us
  transfers between devices with their start and end apart: 4, of which 4 were waited for; matrix products, arithmetic and copies ran while one was open for 2% of the time, Pallas kernels for 0%

commit v1 on v0

v1 whole, which is shorter than its diff:
```python
import functools

import jax
import jax.numpy as jnp
from jax import lax
from jax.experimental import pallas as pl
from jax.experimental.pallas import tpu as pltpu
from jax.sharding import PartitionSpec as P

SEPARATIONS = (-2, -1, 1, 2)


def contract_kernel(items, where_ref, table_ref, sources_ref, cosine_ref, sine_ref, *refs):
    sink_refs, out_ref, block_ref = refs[:items], refs[items], refs[items + 1]
    ops, _, dim, _ = sources_ref.shape
    slots = out_ref.shape[1]
    out_ref[...] = jnp.zeros_like(out_ref)

    for item in range(items):
        start = where_ref[2 * item] * (3 * slots)
        number = where_ref[2 * item + 1]

        def wanted(slot):
            pick = table_ref[start + slot]
            live = table_ref[start + 2 * slots + slot] >= 0
            return jnp.logical_and(live, pick // ops == number)

        some = functools.reduce(jnp.logical_or, [wanted(slot) for slot in range(slots)])

        @pl.when(some)
        def _():
            sink = sink_refs[item]
            block_ref[:dim, :dim] = sink[0]
            block_ref[:dim, dim:] = sink[1]
            block_ref[dim:, :dim] = -sink[1]
            block_ref[dim:, dim:] = sink[0]

            def one(slot, carry):
                @pl.when(wanted(slot))
                def _():
                    op = table_ref[start + slot] % ops
                    moment = table_ref[start + slots + slot]
                    source = jnp.concatenate([sources_ref[op, 0], sources_ref[op, 1]], axis=1)
                    quark = jnp.dot(source, block_ref[...], preferred_element_type=jnp.float32)
                    quark_real, quark_imag = quark[:, :dim], quark[:, dim:]
                    cosine, sine = cosine_ref[moment], sine_ref[moment]
                    phased = jnp.concatenate(
                        [
                            (quark_real * cosine - quark_imag * sine).astype(jnp.bfloat16),
                            (quark_real * sine + quark_imag * cosine).astype(jnp.bfloat16),
                        ],
                        axis=1,
                    )
                    loop = lax.dot_general(
                        phased, block_ref[...], (((1,), (1,)), ((), ())), preferred_element_type=jnp.float32
                    )
                    loop_real, loop_imag = loop[:, :dim], loop[:, dim:]
                    real_t, imag_t = loop_real.T, loop_imag.T
                    scale = 1.0 / dim
                    out_ref[item, slot, 0:1] = scale * jnp.sum(
                        loop_real * real_t - loop_imag * imag_t, axis=0, keepdims=True
                    )
                    out_ref[item, slot, 1:2] = scale * jnp.sum(
                        loop_real * imag_t + loop_imag * real_t, axis=0, keepdims=True
                    )

                return carry

            lax.fori_loop(0, slots, one, 0)


def contract(where, table, sources, cosine, sine, sinks):
    items = len(sinks)
    dim = sources.shape[-1]
    slots = table.shape[-1]
    vmem = pl.BlockSpec(memory_space=pltpu.VMEM)
    smem = pl.BlockSpec(memory_space=pltpu.SMEM)
    return pl.pallas_call(
        functools.partial(contract_kernel, items),
        out_shape=jax.ShapeDtypeStruct((items, slots, 2, dim), jnp.float32),
        in_specs=[smem, smem] + [vmem] * (3 + items),
        out_specs=vmem,
        scratch_shapes=[pltpu.VMEM((2 * dim, 2 * dim), jnp.bfloat16)],
        name=f"contract_{items}",
    )(where, table.reshape(-1), sources, cosine, sine, *sinks)


def shift(values, by):
    length = lax.axis_size("tm")
    return lax.ppermute(values, "tm", [(i, (i + by) % length) for i in range(length)])


def direct(run, sink):
    me = lax.axis_index("tm")
    length = lax.axis_size("tm")
    total = None
    for number, separation in enumerate(SEPARATIONS):
        where = jnp.stack([(me - separation) % length, number])
        values = shift(run(where, [shift(sink, separation)])[0], -separation)
        total = values if total is None else total + values
    return total


def relayed(run, sink):
    me = lax.axis_index("tm")
    length = lax.axis_size("tm")
    planes = lax.axis_size("op")
    core, pair = me % 2, me // 2

    def exchange(values, moves):
        pairs = [
            (t * planes + z, u * planes + w)
            for t in range(length)
            for z in range(planes)
            for u, w in [moves(t, z)]
            if u is not None
        ]
        return lax.ppermute(values, ("tm", "op"), pairs)

    near = lambda t, z: (t + z) % 2 == 0
    partner = exchange(sink, lambda t, z: (t ^ 1, z))
    first = exchange(sink, lambda t, z: (t ^ 2, z) if near(t, z) else (t ^ 4, z))
    across = exchange(first, lambda t, z: (t ^ 4, z) if near(t, z) else (t ^ 2, z))
    other = exchange(first, lambda t, z: (t, z ^ 1) if near(t, z) else (None, None))
    beside = jnp.where(near(me, lax.axis_index("op")), first, other)
    lends_beside = (pair + core) % 2 == 0
    lent = exchange(jnp.where(lends_beside, beside, across), lambda t, z: (t ^ 1, z))

    even = pair % 2 == 0
    up, down = (me + 2) % length, (me - 2) % length
    where_partner = jnp.stack([me ^ 1, 1 + core])
    where_direct = jnp.stack([me ^ 2, jnp.where(even, 0, 3), me ^ 6, jnp.where(even, 3, 0)])
    where_lent = jnp.stack([jnp.where(core == 0, me - 1, me + 1) % length, 2 - core])

    values_partner = exchange(run(where_partner, [partner])[0], lambda t, z: (t ^ 1, z))
    values = run(where_direct, [beside, across])
    values_beside = exchange(values[0], lambda t, z: (t ^ 2, z))
    values_across = exchange(values[1], lambda t, z: (t ^ 6, z))
    values_lent = exchange(
        run(where_lent, [lent])[0], lambda t, z: ((t + 1 if t % 2 else t - 1) % length, z)
    )
    return values_partner + values_beside + values_across + values_lent


def shards(sources, sink, phase, task_table):
    table = lax.all_gather(task_table[:, 0], "tm")
    cosine = jnp.cos(phase)[:, None, :]
    sine = jnp.sin(phase)[:, None, :]

    def run(where, sinks):
        return contract(where.astype(jnp.int32), table, sources[0], cosine, sine, sinks)

    pairs = lax.axis_size("tm") // 2
    method = relayed if pairs == 4 and lax.axis_size("op") % 2 == 0 else direct
    return method(run, sink[0])[None]


def solution(mesh):
    return jax.shard_map(
        shards,
        mesh=mesh,
        in_specs=(
            P(("grp", "tm"), "op", None, None, None),
            P(("grp", "tm"), None, None, None),
            P(),
            P(None, ("grp", "tm"), "op"),
        ),
        out_specs=P(("grp", "tm"), "op", None, None),
        check_vma=False,
    )
```

time: 149 us -> 63.9 us (0.43)
  the two profiles are of different devices: /device:TPU:1 before, /device:TPU:0 now
where the time goes in v1:
time: 63.9 us; the launch traced here: 64.3 us
  waiting for transfers between devices  19.5 us (31%)
  starting transfers between devices  17.6 us (28%)
  Pallas kernels  9.29 us (15%)
  blocking collectives  8.92 us (14%)
  local copies, waits for them, and re-layouts  4.79 us (7%)
  other arithmetic  4.05 us (6%)
    ppermute x9, waiting for transfers between devices, exchange(): return lax.ppermute(values, ('tm', 'op'), pairs)  19.5 us
    ppermute x9, starting transfers between devices, exchange(): return lax.ppermute(values, ('tm', 'op'), pairs)  17.6 us
    pallas_call x3, Pallas kernels, contract(): pl.pallas_call(functools.partial(contract_kernel, items), out_shape=jax.S...  9.29 us
    all_gather x1, blocking collectives, shards(): table = lax.all_gather(task_table[:, 0], 'tm')  8.92 us
    unnamed x10, local copies, waits for them, and re-layouts  1.67 us
  transfers between devices with their start and end apart: 9, of which 4 were waited for; matrix products, arithmetic and copies ran while one was open for 10% of the time, Pallas kernels for 14%

profile of v1, /device:TPU:0, one launch (start us, length us, event | category | flops | bytes accessed | tf_op | source)
XLA Modules:
  0.0 64.3 jit_solution(4105189082411726137)
XLA Ops:
  0.0 3.0 %collective-permute-start.2 = (bf16[2,384,384]{2,1,0:T(8,128)(2,1)}, bf16[2,384,384]{2,1,0:T(8,128)(2,1)S(1)}, u32[]{:S(2)}, u32[]{:S(2)}) collective-permute-start(bf16[2,384,384]{2,1,0:T(8,128)(2,1)} %bitcast.23), channel_id=1, source_target_pairs={{0,8},{1,17},{2,10},{3,19},{4,20},{5,13},{6,22},{7,15},{8,0},{9,25... | collective-permute-start | bytes 1769480 | tf_op jit(solution)/shard_map/ppermute | solution.py:118
  3.0 8.1 %collective-permute-done.2 = bf16[2,384,384]{2,1,0:T(8,128)(2,1)S(1)} collective-permute-done((bf16[2,384,384]{2,1,0:T(8,128)(2,1)}, bf16[2,384,384]{2,1,0:T(8,128)(2,1)S(1)}, u32[]{:S(2)}, u32[]{:S(2)}) %collective-permute-start.2) | collective-permute-done | bytes 589856 | tf_op jit(solution)/shard_map/ppermute | solution.py:118
  11.0 2.1 %collective-permute-start.4 = (bf16[2,384,384]{2,1,0:T(8,128)(2,1)S(1)}, bf16[2,384,384]{2,1,0:T(8,128)(2,1)S(1)}, u32[]{:S(2)}, u32[]{:S(2)}) collective-permute-start(bf16[2,384,384]{2,1,0:T(8,128)(2,1)S(1)} %collective-permute-done.2), channel_id=1, source_target_pairs={{0,16},{1,9},{2,18},{3,11},{4,12},{5,21},{6,14},{7,23},{8,24},{9,1... | collective-permute-start | bytes 1769480 | tf_op jit(solution)/shard_map/ppermute | solution.py:118
  13.1 3.5 %collective-permute-start.3 = (bf16[2,384,384]{2,1,0:T(8,128)(2,1)S(1)}, bf16[2,384,384]{2,1,0:T(8,128)(2,1)S(1)}, u32[]{:S(2)}, u32[]{:S(2)}) collective-permute-start(bf16[2,384,384]{2,1,0:T(8,128)(2,1)S(1)} %collective-permute-done.2), channel_id=1, source_target_pairs={{0,1},{2,3},{5,4},{7,6},{8,9},{10,11},{13,12},{15,14},{16,17},{18,... | collective-permute-start | bytes 1769480 | tf_op jit(solution)/shard_map/ppermute | solution.py:118
  16.7 4.2 %collective-permute-done.4.refs_1_ = bf16[2,384,384]{2,1,0:T(8,128)(2,1)S(1)} collective-permute-done((bf16[2,384,384]{2,1,0:T(8,128)(2,1)S(1)}, bf16[2,384,384]{2,1,0:T(8,128)(2,1)S(1)}, u32[]{:S(2)}, u32[]{:S(2)}) %collective-permute-start.4) | collective-permute-done | bytes 589856 | tf_op jit(solution)/shard_map/ppermute | solution.py:118
  21.0 3.0 %collective-permute-done.3 = bf16[2,384,384]{2,1,0:T(8,128)(2,1)S(1)} collective-permute-done((bf16[2,384,384]{2,1,0:T(8,128)(2,1)S(1)}, bf16[2,384,384]{2,1,0:T(8,128)(2,1)S(1)}, u32[]{:S(2)}, u32[]{:S(2)}) %collective-permute-start.3) | collective-permute-done | bytes 589856 | tf_op jit(solution)/shard_map/ppermute | solution.py:118
  23.9 0.9 %broadcast_select_fusion = (bf16[2,384,384]{2,1,0:T(8,128)(2,1)S(1)}, bf16[2,384,384]{2,1,0:T(8,128)(2,1)}) fusion(bf16[2,384,384]{2,1,0:T(8,128)(2,1)S(1)} %collective-permute-done.4.refs_1_, pred[]{:T(512)S(6)} %eq.21, bf16[2,384,384]{2,1,0:T(8,128)(2,1)S(1)} %collective-permute-done.2, bf16[2,384,384]{2,1,0:T(8,128)(2,1)S(1)} %collective-permute-done.3, ...), kind=kLoop, calls=%fused_computation | loop fusion | flops 589824 | bytes 2949122 | tf_op jit(solution)/shard_map/jit(_where)/select_n | solution.py:127
  25.0 0.6 broadcast_in_dim.10.sine_ref
  25.6 0.6 broadcast_in_dim.9.cosine_ref
  26.2 8.9 %all-gather = s32[24,1,4]{2,1,0:T(1,128)S(1)} all-gather(s32[3,1,4]{2,1,0:T(1,128)S(1)} %copy-done.4), channel_id=2, replica_groups=mesh['grp'=1,'tm'=8,'op'=4] {'tm'}, dimensions={0}, use_global_device_ids=true | all-gather | bytes 432 | tf_op jit(solution)/shard_map/all_gather | solution.py:146
  35.6 0.7 %reduce.3 = s32[24,4]{1,0:T(8,128)S(1)} reduce(s32[24,1,4]{2,1,0:T(1,128)S(1)} %all-gather, s32[]{:T(128)} %broadcast.9), dimensions={1}, to_apply=%all-gather.reduce_sub_computation.3 | reduce | bytes 772 | tf_op jit(solution)/shard_map/all_gather | solution.py:146
  36.9 0.7 %pad_add_fusion.2.where_ref = s32[2]{0:T(128)} fusion(s32[1]{0:T(128)} %bitcast.12, s32[1]{0:T(128)} %bitcast.11), kind=kLoop, calls=%fused_computation.7 | loop fusion | flops 2 | bytes 16 | tf_op jit(solution)/shard_map/stack | solution.py:133
  37.6 0.6 pad_add_fusion.where_ref
  38.2 0.6 pad_add_fusion.1.where_ref
  38.7 0.8 %copy-done.1 = bf16[2,384,384]{2,1,0:T(8,128)(2,1)} copy-done((bf16[2,384,384]{2,1,0:T(8,128)(2,1)}, bf16[2,384,384]{2,1,0:T(8,128)(2,1)S(1)}, u32[]{:S(2)}) %copy-start.1) | copy-done | bytes 589848
  39.6 2.5 %contract_1.2 = f32[1,4,2,384]{3,2,1,0:T(2,128)} custom-call(s32[2]{0:T(128)} %pad_add_fusion.where_ref, s32[96]{0:T(128)} %reshape.2.table_ref, bf16[4,2,384,384]{3,2,1,0:T(8,128)(2,1)} %bitcast.18, f32[8,1,384]{2,1,0:T(1,128)} %broadcast_in_dim.9.cosine_ref, f32[8,1,384]{2,1,0:T(1,128)} %broadcast_in_dim.10.sine_ref, bf16[2,384,384]{2,1,0:T(8,128)(2,1)} %copy-done.1), custom_call_target="tpu_custom_call" | custom-call | tf_op jit(solution)/shard_map/contract_1/pallas_call | solution.py:78
  42.4 2.7 %contract_2.1 = f32[2,4,2,384]{3,2,1,0:T(2,128)} custom-call(s32[4]{0:T(128)} %pad_add_fusion.1.where_ref, s32[96]{0:T(128)} %reshape.2.table_ref, bf16[4,2,384,384]{3,2,1,0:T(8,128)(2,1)} %bitcast.19, f32[8,1,384]{2,1,0:T(1,128)} %broadcast_in_dim.9.cosine_ref, f32[8,1,384]{2,1,0:T(1,128)} %broadcast_in_dim.10.sine_ref, ...), custom_call_target="tpu_custom_call" | custom-call | tf_op jit(solution)/shard_map/contract_2/pallas_call | solution.py:78
  45.1 0.7 %slice_bitcast_fusion.1 = (f32[4,2,384]{2,1,0:T(2,128)S(1)}, f32[4,2,384]{2,1,0:T(2,128)S(1)}) fusion(f32[2,4,2,384]{3,2,1,0:T(2,128)} %contract_2.1), kind=kLoop, calls=%fused_computation.3 | loop fusion | bytes 49152 | tf_op jit(solution)/shard_map/squeeze | solution.py:137
  45.8 7.1 %collective-permute-start.5 = (f32[4,2,384]{2,1,0:T(2,128)S(1)}, f32[4,2,384]{2,1,0:T(2,128)S(1)}, u32[]{:S(2)}, u32[]{:S(2)}) collective-permute-start(f32[4,2,384]{2,1,0:T(2,128)S(1)} %get-tuple-element.7), channel_id=1, source_target_pairs={{0,8},{1,9},{2,10},{3,11},{4,12},{5,13},{6,14},{7,15},{8,0},{9,1},... | collective-permute-start | bytes 36872 | tf_op jit(solution)/shard_map/ppermute | solution.py:118
  52.8 1.6 %collective-permute-start.6 = (f32[4,2,384]{2,1,0:T(2,128)S(1)}, f32[4,2,384]{2,1,0:T(2,128)S(1)}, u32[]{:S(2)}, u32[]{:S(2)}) collective-permute-start(f32[4,2,384]{2,1,0:T(2,128)S(1)} %get-tuple-element.8), channel_id=1, source_target_pairs={{0,24},{1,25},{2,26},{3,27},{4,28},{5,29},{6,30},{7,31},{8,16},{9,... | collective-permute-start | bytes 36872 | tf_op jit(solution)/shard_map/ppermute | solution.py:118
  54.5 0.8 %copy-done.2 = bf16[2,384,384]{2,1,0:T(8,128)(2,1)} copy-done((bf16[2,384,384]{2,1,0:T(8,128)(2,1)}, bf16[2,384,384]{2,1,0:T(8,128)(2,1)S(1)}, u32[]{:S(2)}) %copy-start.2) | copy-done | bytes 589848
  55.3 4.2 %contract_1.3 = f32[1,4,2,384]{3,2,1,0:T(2,128)} custom-call(s32[2]{0:T(128)} %pad_add_fusion.2.where_ref, s32[96]{0:T(128)} %reshape.2.table_ref, bf16[4,2,384,384]{3,2,1,0:T(8,128)(2,1)} %bitcast.20, f32[8,1,384]{2,1,0:T(1,128)} %broadcast_in_dim.9.cosine_ref, f32[8,1,384]{2,1,0:T(1,128)} %broadcast_in_dim.10.sine_ref, bf16[2,384,384]{2,1,0:T(8,128)(2,1)} %copy-done.2), custom_call_target="tpu_custom_call" | custom-call | tf_op jit(solution)/shard_map/contract_1/pallas_call | solution.py:78
  59.5 4.2 %collective-permute-done.8 = f32[4,2,384]{2,1,0:T(2,128)S(1)} collective-permute-done((f32[4,2,384]{2,1,0:T(2,128)}, f32[4,2,384]{2,1,0:T(2,128)S(1)}, u32[]{:S(2)}, u32[]{:S(2)}) %collective-permute-start.8) | collective-permute-done | bytes 12320 | tf_op jit(solution)/shard_map/ppermute | solution.py:118
  63.7 0.6 add_bitcast_fusion
  (20 shorter events, 1.6 us)
Async XLA Ops:
  0.0 24.9 %copy-start.3 = (f32[8,384]{1,0:T(8,128)S(1)}, f32[8,384]{1,0:T(8,128)}, u32[]{:S(2)}) copy-start(f32[8,384]{1,0:T(8,128)} %param.6) | copy-start | bytes 36868
  0.0 26.2 %copy-start.4 = (s32[3,1,4]{2,1,0:T(1,128)S(1)}, s32[3,1,4]{2,1,0:T(1,128)}, u32[]{:S(2)}) copy-start(s32[3,1,4]{2,1,0:T(1,128)} %param.7) | copy-start | bytes 148
  0.0 11.0 %collective-permute-start.2 = (bf16[2,384,384]{2,1,0:T(8,128)(2,1)}, bf16[2,384,384]{2,1,0:T(8,128)(2,1)S(1)}, u32[]{:S(2)}, u32[]{:S(2)}) collective-permute-start(bf16[2,384,384]{2,1,0:T(8,128)(2,1)} %bitcast.23), channel_id=1, source_target_pairs={{0,8},{1,17},{2,10},{3,19},{4,20},{5,13},{6,22},{7,15},{8,0},{9,25... | collective-permute-start | bytes 1769480 | tf_op jit(solution)/shard_map/ppermute | solution.py:118
  11.0 9.9 %collective-permute-start.4 = (bf16[2,384,384]{2,1,0:T(8,128)(2,1)S(1)}, bf16[2,384,384]{2,1,0:T(8,128)(2,1)S(1)}, u32[]{:S(2)}, u32[]{:S(2)}) collective-permute-start(bf16[2,384,384]{2,1,0:T(8,128)(2,1)S(1)} %collective-permute-done.2), channel_id=1, source_target_pairs={{0,16},{1,9},{2,18},{3,11},{4,12},{5,21},{6,14},{7,23},{8,24},{9,1... | collective-permute-start | bytes 1769480 | tf_op jit(solution)/shard_map/ppermute | solution.py:118
  13.1 10.8 %collective-permute-start.3 = (bf16[2,384,384]{2,1,0:T(8,128)(2,1)S(1)}, bf16[2,384,384]{2,1,0:T(8,128)(2,1)S(1)}, u32[]{:S(2)}, u32[]{:S(2)}) collective-permute-start(bf16[2,384,384]{2,1,0:T(8,128)(2,1)S(1)} %collective-permute-done.2), channel_id=1, source_target_pairs={{0,1},{2,3},{5,4},{7,6},{8,9},{10,11},{13,12},{15,14},{16,17},{18,... | collective-permute-start | bytes 1769480 | tf_op jit(solution)/shard_map/ppermute | solution.py:118
  16.6 22.2 %collective-permute-start = (bf16[2,384,384]{2,1,0:T(8,128)(2,1)}, bf16[2,384,384]{2,1,0:T(8,128)(2,1)S(1)}, u32[]{:S(2)}, u32[]{:S(2)}) collective-permute-start(bf16[2,384,384]{2,1,0:T(8,128)(2,1)} %bitcast.24), channel_id=1, source_target_pairs={{0,4},{1,5},{2,6},{3,7},{4,0},{5,1},{6,2},{7,3},{8,12},{9,13},{10,... | collective-permute-start | bytes 1769480 | tf_op jit(solution)/shard_map/ppermute | solution.py:118
  21.0 21.1 %copy-start = (bf16[2,384,384]{2,1,0:T(8,128)(2,1)}, bf16[2,384,384]{2,1,0:T(8,128)(2,1)S(1)}, u32[]{:S(2)}) copy-start(bf16[2,384,384]{2,1,0:T(8,128)(2,1)S(1)} %collective-permute-done.4.refs_1_) | copy-start | bytes 1769476
  24.9 29.6 %collective-permute-start.7 = (bf16[2,384,384]{2,1,0:T(8,128)(2,1)S(1)}, bf16[2,384,384]{2,1,0:T(8,128)(2,1)S(1)}, u32[]{:S(2)}, u32[]{:S(2)}) collective-permute-start(bf16[2,384,384]{2,1,0:T(8,128)(2,1)S(1)} %get-tuple-element.5), channel_id=1, source_target_pairs={{0,4},{1,5},{2,6},{3,7},{4,0},{5,1},{6,2},{7,3},{8,12},{9,13},{10,... | collective-permute-start | bytes 1769480 | tf_op jit(solution)/shard_map/ppermute | solution.py:118
  38.7 0.8 %copy-start.1 = (bf16[2,384,384]{2,1,0:T(8,128)(2,1)}, bf16[2,384,384]{2,1,0:T(8,128)(2,1)S(1)}, u32[]{:S(2)}) copy-start(bf16[2,384,384]{2,1,0:T(8,128)(2,1)S(1)} %collective-permute-done.refs_0_) | copy-start | bytes 1769476
  42.0 17.4 %collective-permute-start.1 = (f32[4,2,384]{2,1,0:T(2,128)}, f32[4,2,384]{2,1,0:T(2,128)S(1)}, u32[]{:S(2)}, u32[]{:S(2)}) collective-permute-start(f32[4,2,384]{2,1,0:T(2,128)} %bitcast.21), channel_id=1, source_target_pairs={{0,4},{1,5},{2,6},{3,7},{4,0},{5,1},{6,2},{7,3},{8,12},{9,13},{10,... | collective-permute-start | bytes 36872 | tf_op jit(solution)/shard_map/ppermute | solution.py:118
  45.8 13.7 %collective-permute-start.5 = (f32[4,2,384]{2,1,0:T(2,128)S(1)}, f32[4,2,384]{2,1,0:T(2,128)S(1)}, u32[]{:S(2)}, u32[]{:S(2)}) collective-permute-start(f32[4,2,384]{2,1,0:T(2,128)S(1)} %get-tuple-element.7), channel_id=1, source_target_pairs={{0,8},{1,9},{2,10},{3,11},{4,12},{5,13},{6,14},{7,15},{8,0},{9,1},... | collective-permute-start | bytes 36872 | tf_op jit(solution)/shard_map/ppermute | solution.py:118
  52.8 6.6 %collective-permute-start.6 = (f32[4,2,384]{2,1,0:T(2,128)S(1)}, f32[4,2,384]{2,1,0:T(2,128)S(1)}, u32[]{:S(2)}, u32[]{:S(2)}) collective-permute-start(f32[4,2,384]{2,1,0:T(2,128)S(1)} %get-tuple-element.8), channel_id=1, source_target_pairs={{0,24},{1,25},{2,26},{3,27},{4,28},{5,29},{6,30},{7,31},{8,16},{9,... | collective-permute-start | bytes 36872 | tf_op jit(solution)/shard_map/ppermute | solution.py:118
  54.5 0.8 %copy-start.2 = (bf16[2,384,384]{2,1,0:T(8,128)(2,1)}, bf16[2,384,384]{2,1,0:T(8,128)(2,1)S(1)}, u32[]{:S(2)}) copy-start(bf16[2,384,384]{2,1,0:T(8,128)(2,1)S(1)} %collective-permute-done.7.refs_0_) | copy-start | bytes 1769476
  59.5 4.2 %collective-permute-start.8 = (f32[4,2,384]{2,1,0:T(2,128)}, f32[4,2,384]{2,1,0:T(2,128)S(1)}, u32[]{:S(2)}, u32[]{:S(2)}) collective-permute-start(f32[4,2,384]{2,1,0:T(2,128)} %bitcast.22), channel_id=1, source_target_pairs={{0,28},{1,29},{2,30},{3,31},{4,8},{5,9},{6,10},{7,11},{8,4},{9,5},... | collective-permute-start | bytes 36872 | tf_op jit(solution)/shard_map/ppermute | solution.py:118
